TPU v7x, 32 devices: a whole 2x2x4 slice. The times are simulated.
32 devices in a mesh: gx: 4 (over y, x), gy: 2 (over core), gz: 4 (over z).
Axes of the slice: x: 2, y: 2, z: 4, core: 2. Of those that a mesh axis runs over, the one named last changes fastest.
Arguments:
- phi_start: float32 [64, 96, 512], P('gx', 'gy', 'gz'), may hold values from -30 to 30
Outputs:
- phi_final: float32 [64, 96, 512], P('gx', 'gy', 'gz')
- residuals: float32 [3], replicated
All inputs are finite; a program needn't handle non-finite values.
Results may differ from a plain program's by a relative error of at most 0.0003.
Values sent between devices are 32-bit elements; how exact they have to be, the bound alone decides.
No kernel may reach another device: no remote copies, remote signals or barrier semaphores. Data moves between devices by JAX's collectives and lax.ppermute only.
A program may use at most 64 MiB of HBM per device.

v0:
```python
import jax
import jax.numpy as jnp
from jax import lax
from jax.sharding import PartitionSpec as P

ITERS = 3
pseudo_step = 0.45


def extended_2(cells, sides, width):
    for axis, dim in sides:
        count = lax.axis_size(axis)
        ends = count - 1
        head = lax.slice_in_dim(cells, 0, width, axis=dim)
        tail = lax.slice_in_dim(cells, cells.shape[dim] - width, cells.shape[dim], axis=dim)
        cells = jnp.concatenate(
            [
                lax.ppermute(tail, axis, [(i, (i + 1) % count) for i in range(ends)]),
                cells,
                lax.ppermute(head, axis, [((i + 1) % count, i) for i in range(ends)]),
            ],
            axis=dim,
        )
    return cells


def smooth_sign(field):
    return field / jnp.sqrt(field * field + 1.0)


def upwind_term(back, fwd, positive):
    plus = jnp.maximum(jnp.maximum(back, 0.0) ** 2, jnp.minimum(fwd, 0.0) ** 2)
    minus = jnp.maximum(jnp.minimum(back, 0.0) ** 2, jnp.maximum(fwd, 0.0) ** 2)
    return jnp.where(positive, plus, minus)


def update(ext, sgn):
    center = ext[1:-1, 1:-1, 1:-1]
    positive = sgn > 0.0
    total = upwind_term(center - ext[:-2, 1:-1, 1:-1], ext[2:, 1:-1, 1:-1] - center, positive)
    total = total + upwind_term(
        center - ext[1:-1, :-2, 1:-1], ext[1:-1, 2:, 1:-1] - center, positive
    )
    total = total + upwind_term(
        center - ext[1:-1, 1:-1, :-2], ext[1:-1, 1:-1, 2:] - center, positive
    )
    return center - pseudo_step * sgn * (jnp.sqrt(total) - 1.0)


def clamp_axis(field, margin, dim, count, place):
    length = field.shape[dim]
    position = lax.broadcasted_iota(jnp.int32, field.shape, dim)
    low_value = lax.slice_in_dim(field, margin, margin + 1, axis=dim)
    high_value = lax.slice_in_dim(field, length - margin - 1, length - margin, axis=dim)
    field = jnp.where((place == 0) & (position < margin), low_value, field)
    return jnp.where((place == count - 1) & (position >= length - margin), high_value, field)


def clamp_edges(field, margin):
    field = clamp_axis(field, margin, 0, lax.axis_size("gx"), lax.axis_index("gx"))
    field = clamp_axis(field, margin, 1, lax.axis_size("gy"), lax.axis_index("gy"))
    return clamp_axis(field, margin, 2, lax.axis_size("gz"), lax.axis_index("gz"))


def crop(field, margin):
    if margin == 0:
        return field
    return field[margin:-margin, margin:-margin, margin:-margin]


def reduce_now(partial_value):
    return lax.psum(partial_value, ("gx", "gy", "gz"))


def local(phi_start):
    partials = []
    extended = extended_2(phi_start, (("gx", 0), ("gy", 1), ("gz", 2)), ITERS)
    extended = clamp_edges(extended, ITERS)
    sign_wide = smooth_sign(extended)
    current = extended
    for step in range(ITERS):
        margin = ITERS - step
        newer = update(current, crop(sign_wide, step + 1))
        difference = crop(newer, margin - 1) - crop(current, margin)
        partials.append(reduce_now(jnp.sum(difference * difference)))
        if margin - 1 > 0:
            newer = clamp_edges(newer, margin - 1)
        current = newer
    stacked = jnp.stack(partials)
    cells = phi_start.shape[0] * phi_start.shape[1] * phi_start.shape[2]
    cells = cells * lax.axis_size("gx") * lax.axis_size("gy") * lax.axis_size("gz")
    residuals = jnp.sqrt(stacked / jnp.float32(cells)) / pseudo_step
    return (current, residuals)


def solution(mesh):
    return jax.shard_map(
        local,
        mesh=mesh,
        in_specs=(P("gx", "gy", "gz"),),
        out_specs=(P("gx", "gy", "gz"), P()),
        check_vma=False,
    )
```

profile of v0, /device:TPU:0, one launch (start us, length us, event | category | flops | bytes accessed | tf_op | source)
XLA Modules:
  0.0 102.0 jit_solution(16079190205514697008)
XLA Ops:
  0.6 1.1 %copy.19 = f32[16,48,128]{2,0,1:T(8,128)S(1)} copy(f32[16,48,128]{2,1,0:T(8,128)} %param.1) | data formatting | bytes 786432 | tf_op args[0]
  1.8 4.9 %collective-permute-start = (f32[3,48,128]{2,0,1:T(4,128)S(1)}, f32[3,48,128]{2,0,1:T(4,128)S(1)}, u32[]{:S(2)}, u32[]{:S(2)}) collective-permute-start(f32[3,48,128]{2,0,1:T(4,128)S(1)} %get-tuple-element.35), channel_id=1, source_target_pairs={{0,8},{8,16},{16,24},{1,9},{9,17},{17,25},{2,10},{10,18},{18,26},{... | collective-permute-start | bytes 221192 | tf_op jit(solution)/shard_map/ppermute | solution.py:18
  6.7 1.3 %collective-permute-start.1 = (f32[3,48,128]{2,0,1:T(4,128)S(1)}, f32[3,48,128]{2,0,1:T(4,128)S(1)}, u32[]{:S(2)}, u32[]{:S(2)}) collective-permute-start(f32[3,48,128]{2,0,1:T(4,128)S(1)} %get-tuple-element.36), channel_id=1, source_target_pairs={{8,0},{16,8},{24,16},{9,1},{17,9},{25,17},{10,2},{18,10},{26,18},{... | collective-permute-start | bytes 221192 | tf_op jit(solution)/shard_map/ppermute | solution.py:20
  8.1 0.6 compare_and_fusion.4
  9.7 0.6 compare_and_fusion.2
  10.3 2.9 %collective-permute-done.1 = f32[3,48,128]{2,0,1:T(4,128)S(1)} collective-permute-done((f32[3,48,128]{2,0,1:T(4,128)S(1)}, f32[3,48,128]{2,0,1:T(4,128)S(1)}, u32[]{:S(2)}, u32[]{:S(2)}) %collective-permute-start.1) | collective-permute-done | bytes 73760 | tf_op jit(solution)/shard_map/ppermute | solution.py:20
  13.2 1.3 %collective-permute-start.2 = (f32[22,3,128]{2,0,1:T(8,128)S(1)}, f32[22,3,128]{2,0,1:T(8,128)S(1)}, u32[]{:S(2)}, u32[]{:S(2)}) collective-permute-start(f32[22,3,128]{2,0,1:T(8,128)S(1)} %get-tuple-element.33), channel_id=1, source_target_pairs={{0,4},{1,5},{2,6},{3,7},{8,12},{9,13},{10,14},{11,15},{16,20},{17,... | collective-permute-start | bytes 101384 | tf_op jit(solution)/shard_map/ppermute | solution.py:18
  14.5 1.3 %collective-permute-start.3 = (f32[22,3,128]{2,0,1:T(8,128)S(1)}, f32[22,3,128]{2,0,1:T(8,128)S(1)}, u32[]{:S(2)}, u32[]{:S(2)}) collective-permute-start(f32[22,3,128]{2,0,1:T(8,128)S(1)} %get-tuple-element.34), channel_id=1, source_target_pairs={{4,0},{5,1},{6,2},{7,3},{12,8},{13,9},{14,10},{15,11},{20,16},{21,... | collective-permute-start | bytes 101384 | tf_op jit(solution)/shard_map/ppermute | solution.py:20
  16.4 1.2 %collective-permute-done.3 = f32[22,3,128]{2,0,1:T(8,128)S(1)} collective-permute-done((f32[22,3,128]{2,0,1:T(8,128)S(1)}, f32[22,3,128]{2,0,1:T(8,128)S(1)}, u32[]{:S(2)}, u32[]{:S(2)}) %collective-permute-start.3) | collective-permute-done | bytes 33824 | tf_op jit(solution)/shard_map/ppermute | solution.py:20
  18.3 3.5 %collective-permute-start.4 = (f32[22,54,3]{1,0,2:T(8,128)S(1)}, f32[22,54,3]{1,0,2:T(8,128)S(1)}, u32[]{:S(2)}, u32[]{:S(2)}) collective-permute-start(f32[22,54,3]{1,0,2:T(8,128)S(1)} %copy.22), channel_id=1, source_target_pairs={{0,1},{1,2},{2,3},{4,5},{5,6},{6,7},{8,9},{9,10},{10,11},{12,13},{... | collective-permute-start | bytes 42776 | tf_op jit(solution)/shard_map/ppermute | solution.py:18
  22.1 1.3 %collective-permute-start.5 = (f32[22,54,3]{1,0,2:T(8,128)S(1)}, f32[22,54,3]{1,0,2:T(8,128)S(1)}, u32[]{:S(2)}, u32[]{:S(2)}) collective-permute-start(f32[22,54,3]{1,0,2:T(8,128)S(1)} %copy.23), channel_id=1, source_target_pairs={{1,0},{2,1},{3,2},{5,4},{6,5},{7,6},{9,8},{10,9},{11,10},{13,12},{... | collective-permute-start | bytes 42776 | tf_op jit(solution)/shard_map/ppermute | solution.py:20
  24.3 3.7 %collective-permute-done.5 = f32[22,54,3]{1,0,2:T(8,128)S(1)} collective-permute-done((f32[22,54,3]{1,0,2:T(8,128)S(1)}, f32[22,54,3]{1,0,2:T(8,128)S(1)}, u32[]{:S(2)}, u32[]{:S(2)}) %collective-permute-start.5) | collective-permute-done | bytes 14288 | tf_op jit(solution)/shard_map/ppermute | solution.py:20
  28.3 0.8 pad_maximum_fusion
  29.2 0.8 select_select_fusion.2
  30.1 1.0 %select_select_fusion.1 = f32[22,54,134]{2,0,1:T(8,128)S(1)} fusion(f32[22,134]{1,0:T(8,128)S(1)} %get-tuple-element.16, f32[22,134]{1,0:T(8,128)S(1)} %get-tuple-element.15, pred[54]{0:T(512)(128)(4,1)S(1)} %get-tuple-element.41, pred[54]{0:T(512)(128)(4,1)S(1)} %get-tuple-element.42, f32[54,134]{1,0:T(8,128)S(1)} %get-tuple-element.37, ...), kind=kLoop, calls=%fused_computation.3 | loop fusion | flops 1591920 | bytes 1355160 | tf_op jit(solution)/shard_map/jit(_where)/select_n | solution.py:56
  32.4 3.3 %rsqrt_multiply_fusion = (f32[22,54,134]{2,0,1:T(8,128)S(1)}, f32[22,54,134]{2,0,1:T(8,128)S(1)}) fusion(f32[22,54]{0,1:T(8,128)S(1)} %bitcast.56, pred[134]{0:T(512)(128)(4,1)} %get-tuple-element.43, f32[22,54]{0,1:T(8,128)S(1)} %bitcast.55, pred[134]{0:T(512)(128)(4,1)} %get-tuple-element.44, f32[22,134]{1,0:T(8,128)S(1)} %get-tuple-element.16, ...), kind=kLoop, calls=%fused_computation.1 | loop fusion | flops 2387880 | bytes 2001700 | tf_op jit(solution)/shard_map/div | solution.py:28
  35.7 3.2 %multiply_subtract_fusion = f32[20,52,132]{2,0,1:T(8,128)S(1)} fusion(f32[22,54,134]{2,0,1:T(8,128)S(1)} %get-tuple-element.12, f32[22,54,134]{2,0,1:T(8,128)S(1)} %get-tuple-element.11), kind=kLoop, calls=%fused_computation.14 | loop fusion | flops 6314880 | bytes 4942080 | tf_op jit(solution)/shard_map/sub | solution.py:47
  38.9 1.0 %fusion.3 = f32[]{:T(128)} fusion(f32[22,54,134]{2,0,1:T(8,128)S(1)} %get-tuple-element.12, f32[20,52,132]{2,0,1:T(8,128)S(1)} %multiply_subtract_fusion), kind=kLoop, calls=%fused_computation.31 | loop fusion | flops 294911 | bytes 786436 | tf_op jit(solution)/shard_map/reduce_sum | solution.py:85
  41.3 1.5 %fusion.8 = (f32[20,52,1]{2,0,1:T(8,128)}, f32[20,52,1]{2,0,1:T(8,128)}) fusion(f32[20,52,132]{2,0,1:T(8,128)S(1)} %select_select_fusion.4), kind=kLoop, calls=%fused_computation.78 | loop fusion | bytes 16640 | tf_op jit(solution)/shard_map/slice | solution.py:54
  42.8 1.5 %copy.42 = f32[20,52,1]{0,1,2:T(8,128)S(1)} copy(f32[20,52,1]{2,0,1:T(8,128)} %get-tuple-element.20) | data formatting | bytes 8320 | tf_op jit(solution)/shard_map/jit(_where)/broadcast_in_dim | solution.py:55
  44.3 1.5 %copy.41 = f32[20,52,1]{0,1,2:T(8,128)S(1)} copy(f32[20,52,1]{2,0,1:T(8,128)} %get-tuple-element.19) | data formatting | bytes 8320 | tf_op jit(solution)/shard_map/jit(_where)/broadcast_in_dim | solution.py:56
  45.8 0.6 select_select_fusion.3
  46.5 3.1 %multiply_subtract_fusion.1 = f32[18,50,130]{2,0,1:T(8,128)S(1)} fusion(f32[20,52,132]{2,0,1:T(8,128)S(1)} %select_select_fusion.3, f32[22,54,134]{2,0,1:T(8,128)S(1)} %get-tuple-element.11), kind=kLoop, calls=%fused_computation.24 | loop fusion | flops 5382000 | bytes 4212000 | tf_op jit(solution)/shard_map/sub | solution.py:47
  49.6 1.0 fusion.1
  51.9 1.2 %fusion.10 = (f32[18,50,1]{2,0,1:T(8,128)}, f32[18,50,1]{2,0,1:T(8,128)}) fusion(f32[18,50,130]{2,0,1:T(8,128)S(1)} %select_select_fusion.7), kind=kLoop, calls=%fused_computation.80 | loop fusion | bytes 14400 | tf_op jit(solution)/shard_map/slice | solution.py:54
  53.2 1.5 %copy.43 = f32[18,50,1]{0,1,2:T(8,128)S(1)} copy(f32[18,50,1]{2,0,1:T(8,128)} %get-tuple-element.25) | data formatting | bytes 7200 | tf_op jit(solution)/shard_map/jit(_where)/broadcast_in_dim | solution.py:56
  54.7 1.5 %copy.44 = f32[18,50,1]{0,1,2:T(8,128)S(1)} copy(f32[18,50,1]{2,0,1:T(8,128)} %get-tuple-element.26) | data formatting | bytes 7200 | tf_op jit(solution)/shard_map/jit(_where)/broadcast_in_dim | solution.py:55
  56.2 0.6 select_select_fusion.6
  56.8 1.6 %multiply_reduce_fusion = (f32[]{:T(128)}, f32[16,48,128]{2,0,1:T(8,128)S(1)}) fusion(f32[18,50,130]{2,0,1:T(8,128)S(1)} %select_select_fusion.6, f32[22,54,134]{2,0,1:T(8,128)S(1)} %get-tuple-element.11), kind=kLoop, calls=%fused_computation.38 | loop fusion | flops 4816895 | bytes 3538948 | tf_op jit(solution)/shard_map/reduce_sum | solution.py:85
  58.4 0.9 copy.38
  59.3 40.2 %all-reduce = (f32[1]{0:T(128)}, f32[1]{0:T(128)}, f32[1]{0:T(128)}) all-reduce(f32[1]{0:T(128)} %bitcast.20, f32[1]{0:T(128)} %bitcast.19, f32[1]{0:T(128)} %bitcast.18), channel_id=1, replica_groups=mesh['gx'=4,'gy'=2,'gz'=4] {'gx','gy','gz'}, use_global_device_ids=true, to_apply=%region_5.6 | all-reduce | flops 3 | bytes 24 | tf_op jit(solution)/shard_map/psum | solution.py:72
  99.5 2.5 %fusion.5 = f32[3]{0:T(128)} fusion(f32[1]{0:T(128)} %get-tuple-element.6, f32[1]{0:T(128)} %get-tuple-element.7, f32[1]{0:T(128)} %get-tuple-element.8), kind=kLoop, calls=%fused_computation.75 | loop fusion | flops 12 | bytes 24 | tf_op jit(solution)/shard_map/div | solution.py:92
  (60 shorter events, 7.9 us)
Async XLA Ops:
  1.8 8.5 %collective-permute-start = (f32[3,48,128]{2,0,1:T(4,128)S(1)}, f32[3,48,128]{2,0,1:T(4,128)S(1)}, u32[]{:S(2)}, u32[]{:S(2)}) collective-permute-start(f32[3,48,128]{2,0,1:T(4,128)S(1)} %get-tuple-element.35), channel_id=1, source_target_pairs={{0,8},{8,16},{16,24},{1,9},{9,17},{17,25},{2,10},{10,18},{18,26},{... | collective-permute-start | bytes 221192 | tf_op jit(solution)/shard_map/ppermute | solution.py:18
  6.7 6.5 %collective-permute-start.1 = (f32[3,48,128]{2,0,1:T(4,128)S(1)}, f32[3,48,128]{2,0,1:T(4,128)S(1)}, u32[]{:S(2)}, u32[]{:S(2)}) collective-permute-start(f32[3,48,128]{2,0,1:T(4,128)S(1)} %get-tuple-element.36), channel_id=1, source_target_pairs={{8,0},{16,8},{24,16},{9,1},{17,9},{25,17},{10,2},{18,10},{26,18},{... | collective-permute-start | bytes 221192 | tf_op jit(solution)/shard_map/ppermute | solution.py:20
  8.0 22.0 %copy-start.4 = (pred[54]{0:T(512)(128)(4,1)}, pred[54]{0:T(512)(128)(4,1)S(1)}, u32[]{:S(2)}) copy-start(pred[54]{0:T(512)(128)(4,1)S(1)} %get-tuple-element.41) | copy-start | bytes 166
  8.1 22.0 %copy-start.5 = (pred[54]{0:T(512)(128)(4,1)}, pred[54]{0:T(512)(128)(4,1)S(1)}, u32[]{:S(2)}) copy-start(pred[54]{0:T(512)(128)(4,1)S(1)} %get-tuple-element.42) | copy-start | bytes 166
  13.2 3.2 %collective-permute-start.2 = (f32[22,3,128]{2,0,1:T(8,128)S(1)}, f32[22,3,128]{2,0,1:T(8,128)S(1)}, u32[]{:S(2)}, u32[]{:S(2)}) collective-permute-start(f32[22,3,128]{2,0,1:T(8,128)S(1)} %get-tuple-element.33), channel_id=1, source_target_pairs={{0,4},{1,5},{2,6},{3,7},{8,12},{9,13},{10,14},{11,15},{16,20},{17,... | collective-permute-start | bytes 101384 | tf_op jit(solution)/shard_map/ppermute | solution.py:18
  14.5 3.1 %collective-permute-start.3 = (f32[22,3,128]{2,0,1:T(8,128)S(1)}, f32[22,3,128]{2,0,1:T(8,128)S(1)}, u32[]{:S(2)}, u32[]{:S(2)}) collective-permute-start(f32[22,3,128]{2,0,1:T(8,128)S(1)} %get-tuple-element.34), channel_id=1, source_target_pairs={{4,0},{5,1},{6,2},{7,3},{12,8},{13,9},{14,10},{15,11},{20,16},{21,... | collective-permute-start | bytes 101384 | tf_op jit(solution)/shard_map/ppermute | solution.py:20
  18.3 5.6 %collective-permute-start.4 = (f32[22,54,3]{1,0,2:T(8,128)S(1)}, f32[22,54,3]{1,0,2:T(8,128)S(1)}, u32[]{:S(2)}, u32[]{:S(2)}) collective-permute-start(f32[22,54,3]{1,0,2:T(8,128)S(1)} %copy.22), channel_id=1, source_target_pairs={{0,1},{1,2},{2,3},{4,5},{5,6},{6,7},{8,9},{9,10},{10,11},{12,13},{... | collective-permute-start | bytes 42776 | tf_op jit(solution)/shard_map/ppermute | solution.py:18
  22.1 5.9 %collective-permute-start.5 = (f32[22,54,3]{1,0,2:T(8,128)S(1)}, f32[22,54,3]{1,0,2:T(8,128)S(1)}, u32[]{:S(2)}, u32[]{:S(2)}) collective-permute-start(f32[22,54,3]{1,0,2:T(8,128)S(1)} %copy.23), channel_id=1, source_target_pairs={{1,0},{2,1},{3,2},{5,4},{6,5},{7,6},{9,8},{10,9},{11,10},{13,12},{... | collective-permute-start | bytes 42776 | tf_op jit(solution)/shard_map/ppermute | solution.py:20
  40.1 0.7 copy-start.2
  40.1 0.7 copy-start.3
  42.8 3.0 %copy-start.8 = (pred[132]{0:T(512)(128)(4,1)S(1)}, pred[132]{0:T(512)(128)(4,1)}, u32[]{:S(2)}) copy-start(pred[132]{0:T(512)(128)(4,1)} %get-tuple-element.49) | copy-start | bytes 400
  42.8 3.0 %copy-start.9 = (pred[132]{0:T(512)(128)(4,1)S(1)}, pred[132]{0:T(512)(128)(4,1)}, u32[]{:S(2)}) copy-start(pred[132]{0:T(512)(128)(4,1)} %get-tuple-element.50) | copy-start | bytes 400
  46.5 4.2 %copy-start = (pred[18]{0:T(512)(128)(4,1)S(1)}, pred[18]{0:T(512)(128)(4,1)}, u32[]{:S(2)}) copy-start(pred[18]{0:T(512)(128)(4,1)} %get-tuple-element.51) | copy-start | bytes 58
  46.5 4.2 %copy-start.1 = (pred[18]{0:T(512)(128)(4,1)S(1)}, pred[18]{0:T(512)(128)(4,1)}, u32[]{:S(2)}) copy-start(pred[18]{0:T(512)(128)(4,1)} %get-tuple-element.52) | copy-start | bytes 58
  50.7 0.7 copy-start.6
  50.7 0.7 copy-start.7
  51.9 4.2 %copy-start.10 = (pred[130]{0:T(512)(128)(4,1)S(1)}, pred[130]{0:T(512)(128)(4,1)}, u32[]{:S(2)}) copy-start(pred[130]{0:T(512)(128)(4,1)} %get-tuple-element.55) | copy-start | bytes 394
  51.9 4.2 %copy-start.11 = (pred[130]{0:T(512)(128)(4,1)S(1)}, pred[130]{0:T(512)(128)(4,1)}, u32[]{:S(2)}) copy-start(pred[130]{0:T(512)(128)(4,1)} %get-tuple-element.56) | copy-start | bytes 394
where the time goes:
time: 102 us
  blocking collectives  40.2 us (39%)
  other arithmetic  24.7 us (24%)
  local copies, waits for them, and re-layouts  14.7 us (14%)
  starting transfers between devices  13.5 us (13%)
  waiting for transfers between devices  7.76 us (8%)
  between operations  1.03 us (1%)
    psum x1, blocking collectives, reduce_now(): return lax.psum(partial_value, ('gx', 'gy', 'gz'))  40.2 us
    ppermute x3, starting transfers between devices, extended_2(): lax.ppermute(tail, axis, [(i, (i + 1) % count) for i in range(ends)])  9.66 us
    ppermute x3, waiting for transfers between devices, extended_2(): lax.ppermute(head, axis, [((i + 1) % count, i) for i in range(ends)])  7.75 us
    sub x2, other arithmetic, update(): return center - pseudo_step * sgn * (jnp.sqrt(total) - 1.0)  6.34 us
    select_n x8, other arithmetic, clamp_axis(): jnp.where((place == count - 1) & (position >= length - margin), high_valu...  4.72 us
    ppermute x3, starting transfers between devices, extended_2(): lax.ppermute(head, axis, [((i + 1) % count, i) for i in range(ends)])  3.88 us
    reduce_sum x3, other arithmetic, local(): partials.append(reduce_now(jnp.sum(difference * difference)))  3.58 us
    broadcast_in_dim x6, local copies, waits for them, and re-layouts, clamp_axis(): jnp.where((place == count - 1) & (position >= length - margin), high_valu...  3.46 us
  transfers between devices with their start and end apart: 6, of which 3 were waited for; matrix products, arithmetic and copies ran while one was open for 4% of the time, Pallas kernels for 0%

commit v1 on v0

--- a/solution.py
+++ b/solution.py
@@ -69,7 +69,7 @@
 
 
 def reduce_now(partial_value):
-    return lax.psum(partial_value, ("gx", "gy", "gz"))
+    return lax.psum(lax.psum(partial_value, ("gy", "gz")), "gx")
 
 
 def local(phi_start):

time: 102 us -> 88.6 us (0.87)
  blocking collectives: 40.2 us -> 26.5 us
    psum x1 -> x2, blocking collectives: 40.2 us -> 26.5 us  [reduce_now(): return lax.psum(lax.psum(partial_value, ('gy', 'gz')), 'gx')]
  transfers between devices with their start and end apart: 6 -> 6, of which waited for: 3 -> 3; matrix products, arithmetic and copies ran while one was open for 4% -> 5% of each run, Pallas kernels for 0% -> 0%
where the time goes in v1:
time: 88.6 us; the launch traced here: 88.1 us
  blocking collectives  26.5 us (30%)
  other arithmetic  24.6 us (28%)
  local copies, waits for them, and re-layouts  14.7 us (17%)
  starting transfers between devices  13.5 us (15%)
  waiting for transfers between devices  7.78 us (9%)
  between operations  1.03 us (1%)
    psum x2, blocking collectives, reduce_now(): return lax.psum(lax.psum(partial_value, ('gy', 'gz')), 'gx')  26.5 us
    ppermute x3, starting transfers between devices, extended_2(): lax.ppermute(tail, axis, [(i, (i + 1) % count) for i in range(ends)])  9.66 us
    ppermute x3, waiting for transfers between devices, extended_2(): lax.ppermute(head, axis, [((i + 1) % count, i) for i in range(ends)])  7.77 us
    sub x2, other arithmetic, update(): return center - pseudo_step * sgn * (jnp.sqrt(total) - 1.0)  6.34 us
    select_n x8, other arithmetic, clamp_axis(): jnp.where((place == count - 1) & (position >= length - margin), high_valu...  4.72 us
    ppermute x3, starting transfers between devices, extended_2(): lax.ppermute(head, axis, [((i + 1) % count, i) for i in range(ends)])  3.88 us
    reduce_sum x3, other arithmetic, local(): partials.append(reduce_now(jnp.sum(difference * difference)))  3.62 us
    broadcast_in_dim x6, local copies, waits for them, and re-layouts, clamp_axis(): jnp.where((place == count - 1) & (position >= length - margin), high_valu...  3.46 us
  transfers between devices with their start and end apart: 6, of which 3 were waited for; matrix products, arithmetic and copies ran while one was open for 5% of the time, Pallas kernels for 0%

profile of v1, /device:TPU:0, one launch (start us, length us, event | category | flops | bytes accessed | tf_op | source)
XLA Modules:
  0.0 88.1 jit_solution(970028498442245687)
XLA Ops:
  0.6 1.1 %copy.19 = f32[16,48,128]{2,0,1:T(8,128)S(1)} copy(f32[16,48,128]{2,1,0:T(8,128)} %param.1) | data formatting | bytes 786432 | tf_op args[0]
  1.8 4.9 %collective-permute-start = (f32[3,48,128]{2,0,1:T(4,128)S(1)}, f32[3,48,128]{2,0,1:T(4,128)S(1)}, u32[]{:S(2)}, u32[]{:S(2)}) collective-permute-start(f32[3,48,128]{2,0,1:T(4,128)S(1)} %get-tuple-element.38), channel_id=1, source_target_pairs={{0,8},{8,16},{16,24},{1,9},{9,17},{17,25},{2,10},{10,18},{18,26},{... | collective-permute-start | bytes 221192 | tf_op jit(solution)/shard_map/ppermute | solution.py:18
  6.7 1.3 %collective-permute-start.1 = (f32[3,48,128]{2,0,1:T(4,128)S(1)}, f32[3,48,128]{2,0,1:T(4,128)S(1)}, u32[]{:S(2)}, u32[]{:S(2)}) collective-permute-start(f32[3,48,128]{2,0,1:T(4,128)S(1)} %get-tuple-element.39), channel_id=1, source_target_pairs={{8,0},{16,8},{24,16},{9,1},{17,9},{25,17},{10,2},{18,10},{26,18},{... | collective-permute-start | bytes 221192 | tf_op jit(solution)/shard_map/ppermute | solution.py:20
  10.3 2.9 %collective-permute-done.1 = f32[3,48,128]{2,0,1:T(4,128)S(1)} collective-permute-done((f32[3,48,128]{2,0,1:T(4,128)S(1)}, f32[3,48,128]{2,0,1:T(4,128)S(1)}, u32[]{:S(2)}, u32[]{:S(2)}) %collective-permute-start.1) | collective-permute-done | bytes 73760 | tf_op jit(solution)/shard_map/ppermute | solution.py:20
  13.2 1.3 %collective-permute-start.2 = (f32[22,3,128]{2,0,1:T(8,128)S(1)}, f32[22,3,128]{2,0,1:T(8,128)S(1)}, u32[]{:S(2)}, u32[]{:S(2)}) collective-permute-start(f32[22,3,128]{2,0,1:T(8,128)S(1)} %get-tuple-element.36), channel_id=1, source_target_pairs={{0,4},{1,5},{2,6},{3,7},{8,12},{9,13},{10,14},{11,15},{16,20},{17,... | collective-permute-start | bytes 101384 | tf_op jit(solution)/shard_map/ppermute | solution.py:18
  14.5 1.3 %collective-permute-start.3 = (f32[22,3,128]{2,0,1:T(8,128)S(1)}, f32[22,3,128]{2,0,1:T(8,128)S(1)}, u32[]{:S(2)}, u32[]{:S(2)}) collective-permute-start(f32[22,3,128]{2,0,1:T(8,128)S(1)} %get-tuple-element.37), channel_id=1, source_target_pairs={{4,0},{5,1},{6,2},{7,3},{12,8},{13,9},{14,10},{15,11},{20,16},{21,... | collective-permute-start | bytes 101384 | tf_op jit(solution)/shard_map/ppermute | solution.py:20
  15.8 0.6 compare_and_fusion.1
  16.4 1.2 %collective-permute-done.3 = f32[22,3,128]{2,0,1:T(8,128)S(1)} collective-permute-done((f32[22,3,128]{2,0,1:T(8,128)S(1)}, f32[22,3,128]{2,0,1:T(8,128)S(1)}, u32[]{:S(2)}, u32[]{:S(2)}) %collective-permute-start.3) | collective-permute-done | bytes 33824 | tf_op jit(solution)/shard_map/ppermute | solution.py:20
  18.3 3.5 %collective-permute-start.4 = (f32[22,54,3]{1,0,2:T(8,128)S(1)}, f32[22,54,3]{1,0,2:T(8,128)S(1)}, u32[]{:S(2)}, u32[]{:S(2)}) collective-permute-start(f32[22,54,3]{1,0,2:T(8,128)S(1)} %copy.22), channel_id=1, source_target_pairs={{0,1},{1,2},{2,3},{4,5},{5,6},{6,7},{8,9},{9,10},{10,11},{12,13},{... | collective-permute-start | bytes 42776 | tf_op jit(solution)/shard_map/ppermute | solution.py:18
  22.1 1.3 %collective-permute-start.5 = (f32[22,54,3]{1,0,2:T(8,128)S(1)}, f32[22,54,3]{1,0,2:T(8,128)S(1)}, u32[]{:S(2)}, u32[]{:S(2)}) collective-permute-start(f32[22,54,3]{1,0,2:T(8,128)S(1)} %copy.23), channel_id=1, source_target_pairs={{1,0},{2,1},{3,2},{5,4},{6,5},{7,6},{9,8},{10,9},{11,10},{13,12},{... | collective-permute-start | bytes 42776 | tf_op jit(solution)/shard_map/ppermute | solution.py:20
  24.3 3.6 %collective-permute-done.5 = f32[22,54,3]{1,0,2:T(8,128)S(1)} collective-permute-done((f32[22,54,3]{1,0,2:T(8,128)S(1)}, f32[22,54,3]{1,0,2:T(8,128)S(1)}, u32[]{:S(2)}, u32[]{:S(2)}) %collective-permute-start.5) | collective-permute-done | bytes 14288 | tf_op jit(solution)/shard_map/ppermute | solution.py:20
  28.3 0.8 pad_maximum_fusion
  29.2 0.8 select_select_fusion.2
  30.1 1.0 %select_select_fusion.1 = f32[22,54,134]{2,0,1:T(8,128)S(1)} fusion(f32[22,134]{1,0:T(8,128)S(1)} %get-tuple-element.19, f32[22,134]{1,0:T(8,128)S(1)} %get-tuple-element.18, pred[54]{0:T(512)(128)(4,1)S(1)} %get-tuple-element.44, pred[54]{0:T(512)(128)(4,1)S(1)} %get-tuple-element.45, f32[54,134]{1,0:T(8,128)S(1)} %get-tuple-element.40, ...), kind=kLoop, calls=%fused_computation.3 | loop fusion | flops 1591920 | bytes 1355160 | tf_op jit(solution)/shard_map/jit(_where)/select_n | solution.py:56
  32.4 3.3 %rsqrt_multiply_fusion = (f32[22,54,134]{2,0,1:T(8,128)S(1)}, f32[22,54,134]{2,0,1:T(8,128)S(1)}) fusion(f32[22,54]{0,1:T(8,128)S(1)} %bitcast.56, pred[134]{0:T(512)(128)(4,1)} %get-tuple-element.46, f32[22,54]{0,1:T(8,128)S(1)} %bitcast.55, pred[134]{0:T(512)(128)(4,1)} %get-tuple-element.47, f32[22,134]{1,0:T(8,128)S(1)} %get-tuple-element.19, ...), kind=kLoop, calls=%fused_computation.1 | loop fusion | flops 2387880 | bytes 2001700 | tf_op jit(solution)/shard_map/div | solution.py:28
  35.7 3.2 %multiply_subtract_fusion = f32[20,52,132]{2,0,1:T(8,128)S(1)} fusion(f32[22,54,134]{2,0,1:T(8,128)S(1)} %get-tuple-element.15, f32[22,54,134]{2,0,1:T(8,128)S(1)} %get-tuple-element.14), kind=kLoop, calls=%fused_computation.14 | loop fusion | flops 6314880 | bytes 4942080 | tf_op jit(solution)/shard_map/sub | solution.py:47
  39.0 1.0 %fusion.3 = f32[]{:T(128)} fusion(f32[22,54,134]{2,0,1:T(8,128)S(1)} %get-tuple-element.15, f32[20,52,132]{2,0,1:T(8,128)S(1)} %multiply_subtract_fusion), kind=kLoop, calls=%fused_computation.31 | loop fusion | flops 294911 | bytes 786436 | tf_op jit(solution)/shard_map/reduce_sum | solution.py:85
  41.3 1.5 %fusion.8 = (f32[20,52,1]{2,0,1:T(8,128)}, f32[20,52,1]{2,0,1:T(8,128)}) fusion(f32[20,52,132]{2,0,1:T(8,128)S(1)} %select_select_fusion.4), kind=kLoop, calls=%fused_computation.78 | loop fusion | bytes 16640 | tf_op jit(solution)/shard_map/slice | solution.py:54
  42.7 1.5 %copy.42 = f32[20,52,1]{0,1,2:T(8,128)S(1)} copy(f32[20,52,1]{2,0,1:T(8,128)} %get-tuple-element.23) | data formatting | bytes 8320 | tf_op jit(solution)/shard_map/jit(_where)/broadcast_in_dim | solution.py:55
  44.3 1.5 %copy.41 = f32[20,52,1]{0,1,2:T(8,128)S(1)} copy(f32[20,52,1]{2,0,1:T(8,128)} %get-tuple-element.22) | data formatting | bytes 8320 | tf_op jit(solution)/shard_map/jit(_where)/broadcast_in_dim | solution.py:56
  45.8 0.6 select_select_fusion.3
  46.4 3.1 %multiply_subtract_fusion.1 = f32[18,50,130]{2,0,1:T(8,128)S(1)} fusion(f32[20,52,132]{2,0,1:T(8,128)S(1)} %select_select_fusion.3, f32[22,54,134]{2,0,1:T(8,128)S(1)} %get-tuple-element.14), kind=kLoop, calls=%fused_computation.24 | loop fusion | flops 5382000 | bytes 4212000 | tf_op jit(solution)/shard_map/sub | solution.py:47
  49.6 1.0 %fusion.1 = f32[]{:T(128)} fusion(f32[20,52,132]{2,0,1:T(8,128)S(1)} %select_select_fusion.3, f32[18,50,130]{2,0,1:T(8,128)S(1)} %multiply_subtract_fusion.1), kind=kLoop, calls=%fused_computation.28 | loop fusion | flops 294911 | bytes 786436 | tf_op jit(solution)/shard_map/reduce_sum | solution.py:85
  51.9 1.2 %fusion.10 = (f32[18,50,1]{2,0,1:T(8,128)}, f32[18,50,1]{2,0,1:T(8,128)}) fusion(f32[18,50,130]{2,0,1:T(8,128)S(1)} %select_select_fusion.7), kind=kLoop, calls=%fused_computation.80 | loop fusion | bytes 14400 | tf_op jit(solution)/shard_map/slice | solution.py:54
  53.1 1.5 %copy.43 = f32[18,50,1]{0,1,2:T(8,128)S(1)} copy(f32[18,50,1]{2,0,1:T(8,128)} %get-tuple-element.28) | data formatting | bytes 7200 | tf_op jit(solution)/shard_map/jit(_where)/broadcast_in_dim | solution.py:56
  54.6 1.5 %copy.44 = f32[18,50,1]{0,1,2:T(8,128)S(1)} copy(f32[18,50,1]{2,0,1:T(8,128)} %get-tuple-element.29) | data formatting | bytes 7200 | tf_op jit(solution)/shard_map/jit(_where)/broadcast_in_dim | solution.py:55
  56.1 0.6 select_select_fusion.6
  56.8 1.6 %multiply_reduce_fusion = (f32[]{:T(128)}, f32[16,48,128]{2,0,1:T(8,128)S(1)}) fusion(f32[18,50,130]{2,0,1:T(8,128)S(1)} %select_select_fusion.6, f32[22,54,134]{2,0,1:T(8,128)S(1)} %get-tuple-element.14), kind=kLoop, calls=%fused_computation.38 | loop fusion | flops 4816895 | bytes 3538948 | tf_op jit(solution)/shard_map/reduce_sum | solution.py:85
  58.4 0.9 copy.38
  59.3 16.0 %all-reduce = (f32[]{:T(128)}, f32[]{:T(128)}, f32[]{:T(128)}) all-reduce(f32[]{:T(128)} %get-tuple-element.12, f32[]{:T(128)} %fusion.1, f32[]{:T(128)} %fusion.3), channel_id=1, replica_groups=mesh['gx'=4,'gy'=2,'gz'=4] {'gy','gz'}, use_global_device_ids=true, to_apply=%region_7.8 | all-reduce | flops 3 | bytes 24 | tf_op jit(solution)/shard_map/psum | solution.py:72
  75.2 10.5 %all-reduce.1 = (f32[1]{0:T(128)}, f32[1]{0:T(128)}, f32[1]{0:T(128)}) all-reduce(f32[1]{0:T(128)} %bitcast.20, f32[1]{0:T(128)} %bitcast.19, f32[1]{0:T(128)} %bitcast.18), channel_id=1, replica_groups=mesh['gx'=4,'gy'=2,'gz'=4] {'gx'}, use_global_device_ids=true, to_apply=%region_8.9 | all-reduce | flops 3 | bytes 24 | tf_op jit(solution)/shard_map/psum | solution.py:72
  85.7 2.4 %fusion.5 = f32[3]{0:T(128)} fusion(f32[1]{0:T(128)} %get-tuple-element.9, f32[1]{0:T(128)} %get-tuple-element.10, f32[1]{0:T(128)} %get-tuple-element.11), kind=kLoop, calls=%fused_computation.75 | loop fusion | flops 12 | bytes 24 | tf_op jit(solution)/shard_map/div | solution.py:92
  (61 shorter events, 8.4 us)
Async XLA Ops:
  1.8 8.5 %collective-permute-start = (f32[3,48,128]{2,0,1:T(4,128)S(1)}, f32[3,48,128]{2,0,1:T(4,128)S(1)}, u32[]{:S(2)}, u32[]{:S(2)}) collective-permute-start(f32[3,48,128]{2,0,1:T(4,128)S(1)} %get-tuple-element.38), channel_id=1, source_target_pairs={{0,8},{8,16},{16,24},{1,9},{9,17},{17,25},{2,10},{10,18},{18,26},{... | collective-permute-start | bytes 221192 | tf_op jit(solution)/shard_map/ppermute | solution.py:18
  6.7 6.5 %collective-permute-start.1 = (f32[3,48,128]{2,0,1:T(4,128)S(1)}, f32[3,48,128]{2,0,1:T(4,128)S(1)}, u32[]{:S(2)}, u32[]{:S(2)}) collective-permute-start(f32[3,48,128]{2,0,1:T(4,128)S(1)} %get-tuple-element.39), channel_id=1, source_target_pairs={{8,0},{16,8},{24,16},{9,1},{17,9},{25,17},{10,2},{18,10},{26,18},{... | collective-permute-start | bytes 221192 | tf_op jit(solution)/shard_map/ppermute | solution.py:20
  8.0 22.0 %copy-start.4 = (pred[54]{0:T(512)(128)(4,1)}, pred[54]{0:T(512)(128)(4,1)S(1)}, u32[]{:S(2)}) copy-start(pred[54]{0:T(512)(128)(4,1)S(1)} %get-tuple-element.44) | copy-start | bytes 166
  8.1 22.0 %copy-start.5 = (pred[54]{0:T(512)(128)(4,1)}, pred[54]{0:T(512)(128)(4,1)S(1)}, u32[]{:S(2)}) copy-start(pred[54]{0:T(512)(128)(4,1)S(1)} %get-tuple-element.45) | copy-start | bytes 166
  13.2 3.2 %collective-permute-start.2 = (f32[22,3,128]{2,0,1:T(8,128)S(1)}, f32[22,3,128]{2,0,1:T(8,128)S(1)}, u32[]{:S(2)}, u32[]{:S(2)}) collective-permute-start(f32[22,3,128]{2,0,1:T(8,128)S(1)} %get-tuple-element.36), channel_id=1, source_target_pairs={{0,4},{1,5},{2,6},{3,7},{8,12},{9,13},{10,14},{11,15},{16,20},{17,... | collective-permute-start | bytes 101384 | tf_op jit(solution)/shard_map/ppermute | solution.py:18
  14.5 3.1 %collective-permute-start.3 = (f32[22,3,128]{2,0,1:T(8,128)S(1)}, f32[22,3,128]{2,0,1:T(8,128)S(1)}, u32[]{:S(2)}, u32[]{:S(2)}) collective-permute-start(f32[22,3,128]{2,0,1:T(8,128)S(1)} %get-tuple-element.37), channel_id=1, source_target_pairs={{4,0},{5,1},{6,2},{7,3},{12,8},{13,9},{14,10},{15,11},{20,16},{21,... | collective-permute-start | bytes 101384 | tf_op jit(solution)/shard_map/ppermute | solution.py:20
  18.3 5.7 %collective-permute-start.4 = (f32[22,54,3]{1,0,2:T(8,128)S(1)}, f32[22,54,3]{1,0,2:T(8,128)S(1)}, u32[]{:S(2)}, u32[]{:S(2)}) collective-permute-start(f32[22,54,3]{1,0,2:T(8,128)S(1)} %copy.22), channel_id=1, source_target_pairs={{0,1},{1,2},{2,3},{4,5},{5,6},{6,7},{8,9},{9,10},{10,11},{12,13},{... | collective-permute-start | bytes 42776 | tf_op jit(solution)/shard_map/ppermute | solution.py:18
  22.1 5.9 %collective-permute-start.5 = (f32[22,54,3]{1,0,2:T(8,128)S(1)}, f32[22,54,3]{1,0,2:T(8,128)S(1)}, u32[]{:S(2)}, u32[]{:S(2)}) collective-permute-start(f32[22,54,3]{1,0,2:T(8,128)S(1)} %copy.23), channel_id=1, source_target_pairs={{1,0},{2,1},{3,2},{5,4},{6,5},{7,6},{9,8},{10,9},{11,10},{13,12},{... | collective-permute-start | bytes 42776 | tf_op jit(solution)/shard_map/ppermute | solution.py:20
  40.1 0.6 copy-start.2
  40.1 0.6 copy-start.3
  42.7 3.0 %copy-start.8 = (pred[132]{0:T(512)(128)(4,1)S(1)}, pred[132]{0:T(512)(128)(4,1)}, u32[]{:S(2)}) copy-start(pred[132]{0:T(512)(128)(4,1)} %get-tuple-element.52) | copy-start | bytes 400
  42.7 3.0 %copy-start.9 = (pred[132]{0:T(512)(128)(4,1)S(1)}, pred[132]{0:T(512)(128)(4,1)}, u32[]{:S(2)}) copy-start(pred[132]{0:T(512)(128)(4,1)} %get-tuple-element.53) | copy-start | bytes 400
  46.4 4.3 %copy-start = (pred[18]{0:T(512)(128)(4,1)S(1)}, pred[18]{0:T(512)(128)(4,1)}, u32[]{:S(2)}) copy-start(pred[18]{0:T(512)(128)(4,1)} %get-tuple-element.54) | copy-start | bytes 58
  46.4 4.3 %copy-start.1 = (pred[18]{0:T(512)(128)(4,1)S(1)}, pred[18]{0:T(512)(128)(4,1)}, u32[]{:S(2)}) copy-start(pred[18]{0:T(512)(128)(4,1)} %get-tuple-element.55) | copy-start | bytes 58
  50.7 0.7 copy-start.6
  50.7 0.7 copy-start.7
  51.9 4.2 %copy-start.10 = (pred[130]{0:T(512)(128)(4,1)S(1)}, pred[130]{0:T(512)(128)(4,1)}, u32[]{:S(2)}) copy-start(pred[130]{0:T(512)(128)(4,1)} %get-tuple-element.58) | copy-start | bytes 394
  51.9 4.2 %copy-start.11 = (pred[130]{0:T(512)(128)(4,1)S(1)}, pred[130]{0:T(512)(128)(4,1)}, u32[]{:S(2)}) copy-start(pred[130]{0:T(512)(128)(4,1)} %get-tuple-element.59) | copy-start | bytes 394
